TPU v7x, 32 devices: a whole 2x2x4 slice. The times are simulated.
32 devices in a mesh: dp: 4 (over x, core), tensor: 8 (over z, y).
Axes of the slice: x: 2, y: 2, z: 4, core: 2. Of those that a mesh axis runs over, the one named last changes fastest.
Arguments:
- attn_ctx: bfloat16 [2048, 8192], P('dp', 'tensor'), may hold values from -6 to 6
- w_out: bfloat16 [8192, 8192], P('tensor'), may hold values from -0.09375 to 0.09375
- resid: bfloat16 [2048, 8192], P(('dp', 'tensor')), may hold values from -6 to 6
- teacher_gain: bfloat16 [8192], replicated, may hold values from 0.25 to 1.75
- dest_row: int32 [2048], replicated, may hold values from 0 to 2047, as said below
- student_in: bfloat16 [2048, 4096], P('dp', 'tensor'), may hold values from -6 to 6
- student_gain: bfloat16 [4096], replicated, may hold values from 0.25 to 1.75
- w_gate: bfloat16 [4096, 14336], P('dp', 'tensor'), may hold values from -0.09375 to 0.09375
- w_up: bfloat16 [4096, 14336], P('dp', 'tensor'), may hold values from -0.09375 to 0.09375
- w_down: bfloat16 [14336, 4096], P('tensor', 'dp'), may hold values from -0.0625 to 0.0625
- proj: bfloat16 [4096, 8192], P('dp', 'tensor'), may hold values from -0.09375 to 0.09375
Outputs:
- student_out: bfloat16 [2048, 4096], P('dp', 'tensor')
- row_loss: float32 [2048], P('dp')
- residue: float32 [2048, 8192], P('dp', 'tensor')
Inputs may be any that keep to these rules, and one draw needn't show every extreme that they name: A permutation of the rows; of the 64 rows i in one aligned block of teacher rows, at most 32 have dest_row[i] in any one tile of 512 student rows, and some tile receives exactly 32 of them.
All inputs are finite; a program needn't handle non-finite values.
Results may differ from a plain program's by a relative error of at most 0.012.
Values may be sent and summed in bfloat16 or wider, within the bound.
A program may use at most 192 MiB of HBM per device.

v0:
```python
import jax
import jax.numpy as jnp
from jax import lax
from jax.sharding import PartitionSpec as P

HT = 8192


def local(
    attn_ctx,
    w_out,
    resid,
    teacher_gain,
    dest_row,
    student_in,
    student_gain,
    w_gate,
    w_up,
    w_down,
    proj,
):
    tensor_count = lax.axis_size("tensor")
    group_count = lax.axis_size("dp")
    tile_rows = attn_ctx.shape[0]
    own_rows = resid.shape[0]
    portion = attn_ctx
    summed = lax.psum_scatter(
        jnp.dot(portion, w_out, preferred_element_type=jnp.float32).astype(jnp.bfloat16),
        "tensor",
        scatter_dimension=0,
        tiled=True,
    ).astype(jnp.float32)
    teacher_hidden = resid.astype(jnp.float32) + summed
    square_mean = jnp.mean(teacher_hidden * teacher_hidden, axis=1, keepdims=True)
    teacher_final = (
        teacher_hidden * lax.rsqrt(square_mean + 1e-06) * teacher_gain.astype(jnp.float32)
    ).astype(jnp.bfloat16)
    capacity = 2 * own_rows // group_count
    source_count = group_count * tensor_count
    group_ids = (dest_row // tile_rows).reshape(source_count, own_rows)
    onehot = (group_ids[:, :, None] == jnp.arange(group_count)[None, None, :]).astype(jnp.int32)
    slot_index = jnp.sum((jnp.cumsum(onehot, 1) - onehot) * onehot, 2)
    my_source = lax.axis_index("dp") * tensor_count + lax.axis_index("tensor")
    own_groups = lax.dynamic_index_in_dim(group_ids, my_source, 0, keepdims=False)
    own_slots = lax.dynamic_index_in_dim(slot_index, my_source, 0, keepdims=False)
    target_slot = own_groups * capacity + own_slots
    selector = (target_slot[None, :] == jnp.arange(group_count * capacity)[:, None]).astype(
        jnp.bfloat16
    )
    packed = jnp.dot(selector, teacher_final, preferred_element_type=jnp.float32).astype(
        jnp.bfloat16
    )
    col_width = teacher_final.shape[1] // tensor_count
    send_blocks = packed.reshape(group_count, capacity, tensor_count, col_width).transpose(
        0, 2, 1, 3
    )
    arrived = lax.all_to_all(
        lax.all_to_all(send_blocks, "dp", split_axis=0, concat_axis=0, tiled=True),
        "tensor",
        split_axis=1,
        concat_axis=1,
        tiled=True,
    )
    flattened = arrived.reshape(source_count * capacity, col_width)
    arrival_index = (jnp.arange(source_count)[:, None] * capacity + slot_index).reshape(-1)
    inverse = jnp.zeros(dest_row.shape, jnp.int32).at[dest_row].set(arrival_index)
    own_arrivals = lax.dynamic_slice_in_dim(inverse, lax.axis_index("dp") * tile_rows, tile_rows, 0)
    target = jnp.take(flattened, own_arrivals, axis=0)
    gathered = lax.all_gather(student_in, "tensor", axis=1, tiled=True)
    x_full = gathered.astype(jnp.float32)
    student_mean = jnp.mean(x_full * x_full, axis=1, keepdims=True)
    normed = (x_full * lax.rsqrt(student_mean + 1e-05) * student_gain.astype(jnp.float32)).astype(
        jnp.bfloat16
    )

    def add_rows(portion):
        return jnp.dot(normed, portion, preferred_element_type=jnp.float32)

    gate_acts = add_rows(lax.all_gather(w_gate, "dp", axis=0, tiled=True))
    up_acts = add_rows(lax.all_gather(w_up, "dp", axis=0, tiled=True))
    hidden = (jax.nn.silu(gate_acts) * up_acts).astype(jnp.bfloat16)
    partial_sum = jnp.dot(
        hidden, lax.all_gather(w_down, "dp", axis=1, tiled=True), preferred_element_type=jnp.float32
    )
    local_cols = student_in.shape[1]
    mlp_sum = lax.psum(partial_sum.astype(jnp.bfloat16), "tensor").astype(jnp.float32)
    out_full = (x_full + mlp_sum).astype(jnp.bfloat16)
    out_local = lax.dynamic_slice_in_dim(
        out_full, lax.axis_index("tensor") * local_cols, local_cols, 1
    )
    pred = jnp.dot(
        out_full, lax.all_gather(proj, "dp", axis=0, tiled=True), preferred_element_type=jnp.float32
    )
    residue = pred - target.astype(jnp.float32)
    row_error = jnp.sum(residue * residue, axis=1)
    row_loss = lax.psum(row_error, "tensor") / HT
    return (out_local, row_loss, residue)


def solution(mesh):
    placed = (
        P("dp", "tensor"),
        P("tensor", None),
        P(("dp", "tensor"), None),
        P(),
        P(),
        P("dp", "tensor"),
        P(),
        P("dp", "tensor"),
        P("dp", "tensor"),
        P("tensor", "dp"),
        P("dp", "tensor"),
    )
    return jax.shard_map(
        local,
        mesh=mesh,
        in_specs=placed,
        out_specs=(P("dp", "tensor"), P("dp"), P("dp", "tensor")),
        check_vma=False,
    )
```

profile of v0, /device:TPU:0, one launch (start us, length us, event | category | flops | bytes accessed | tf_op | source)
XLA Modules:
  0.0 813.1 jit_solution(8429802727703756237)
XLA Ops:
  7.2 0.7 all-gather.6.cloned.1.call-update
  8.0 0.7 all-gather.8.cloned.1.call-update
  8.7 0.7 all-gather.12.cloned.1.call-update
  10.0 16.8 %convolution_convert_fusion = bf16[512,8192]{1,0:T(8,128)(2,1)} fusion(bf16[512,1024]{1,0:T(8,128)(2,1)S(1)} %copy-done, bf16[1024,8192]{1,0:T(8,128)(2,1)} %param.12), kind=kOutput, calls=%fused_computation.5 | convolution fusion | flops 8594128896 | bytes 26214400 | tf_op jit(solution)/shard_map/dot_general | solution.py:28
  27.5 59.9 %all-gather.6.cloned.1.call-done = bf16[512,4096]{1,0:T(8,128)(2,1)} async-done(((bf16[512,512]{1,0:T(8,128)(2,1)}), bf16[512,4096]{1,0:T(8,128)(2,1)}) %all-gather.6.cloned.1.call-update) | async-done | bytes 4194320 | tf_op jit(solution)/shard_map/all_gather | solution.py:69
  87.4 3.1 fusion
  90.5 90.7 %all-gather.8.cloned.1.call-done = bf16[4096,1792]{1,0:T(8,128)(2,1)} async-done(((bf16[1024,1792]{1,0:T(8,128)(2,1)}), bf16[4096,1792]{1,0:T(8,128)(2,1)}) %all-gather.8.cloned.1.call-update) | async-done | bytes 14680080 | tf_op jit(solution)/shard_map/all_gather | solution.py:79
  181.2 14.7 %fusion.11 = f32[512,1792]{1,0:T(8,128)} fusion(bf16[4096,1792]{1,0:T(8,128)(2,1)} %all-gather.8.cloned.1.call-done, bf16[512,4096]{1,0:T(8,128)(2,1)} %all-gather.6.cloned.1.call-done, f32[4096]{0:T(1024)S(1)} %convert_element_type.47, f32[512]{0:T(512)S(1)} %add_rsqrt_fusion), kind=kOutput, calls=%fused_computation.23 | convolution fusion | flops 7524581376 | bytes 22562816 | tf_op jit(solution)/shard_map/dot_general | solution.py:77
  195.8 80.9 %all-gather.12.cloned.1.call-done = bf16[1792,4096]{1,0:T(8,128)(2,1)} async-done(((bf16[1792,1024]{1,0:T(8,128)(2,1)}), bf16[1792,4096]{1,0:T(8,128)(2,1)}) %all-gather.12.cloned.1.call-update) | async-done | bytes 14680080 | tf_op jit(solution)/shard_map/all_gather | solution.py:83
  276.8 95.4 %all-gather.10.cloned.1.call-done = bf16[4096,1792]{1,0:T(8,128)(2,1)} async-done(((bf16[1024,1792]{1,0:T(8,128)(2,1)}), bf16[4096,1792]{1,0:T(8,128)(2,1)}) %all-gather.10.cloned.1.call-update) | async-done | bytes 14680080 | tf_op jit(solution)/shard_map/all_gather | solution.py:80
  372.2 28.8 %convolution_convert_fusion.2 = bf16[512,4096]{1,0:T(8,128)(2,1)} fusion(bf16[1792,4096]{1,0:T(8,128)(2,1)} %all-gather.12.cloned.1.call-done, f32[512,1792]{1,0:T(8,128)} %fusion.11, bf16[4096,1792]{1,0:T(8,128)(2,1)} %all-gather.10.cloned.1.call-done, bf16[512,4096]{1,0:T(8,128)(2,1)} %all-gather.6.cloned.1.call-done, f32[4096]{0:T(1024)S(1)} %convert_element_type.47, ...), kind=kOutput, calls=%fused_computation.11 | convolution fusion | flops 15048376320 | bytes 41437184 | tf_op jit(solution)/shard_map/dot_general | solution.py:82
  402.0 1.7 select_reduce_fusion
  403.9 119.3 %reduce-scatter.2.cloned.1.call-done = bf16[64,8192]{1,0:T(8,128)(2,1)} async-done(((bf16[512,8192]{1,0:T(8,128)(2,1)}), bf16[64,8192]{1,0:T(8,128)(2,1)}) %reduce-scatter.2.cloned.1.call-update) | async-done | bytes 1048592 | tf_op jit(solution)/shard_map/reduce_scatter | solution.py:27
  523.2 1.7 multiply_reduce_fusion.1
  524.9 2.0 convolution_convert_fusion.1
  526.9 1.4 copy.35
  528.3 1.2 copy.37
  529.5 28.2 %all_to_all.10 = bf16[4,8,32,1024]{3,2,1,0:T(8,128)(2,1)S(1)} all-to-all(bf16[4,8,32,1024]{3,2,1,0:T(8,128)(2,1)S(1)} %bitcast.17), channel_id=1, replica_groups=mesh['dp'=4,'tensor'=8] {'dp'}, dimensions={0} | all-to-all | bytes 4194304 | tf_op jit(solution)/shard_map/all_to_all | solution.py:58
  557.7 1.5 copy.33
  559.1 4.3 all-to-all-start.1
  563.7 8.3 %scatter_custom_fusion = s32[2048]{0:T(1024)S(1)} fusion(s32[2048]{0:T(1024)S(1)} %get-tuple-element.5, s32[2048]{0:T(1024)S(1)} %reshape.60, s32[]{:T(128)} %constant.62.clone.1), kind=kCustom, calls=%fused_computation.43 | custom fusion | bytes 8196 | tf_op jit(solution)/shard_map/scatter | solution.py:66
  572.1 64.3 %all-to-all-done.1 = bf16[4,8,32,1024]{3,2,0,1:T(8,128)(2,1)} async-done(((bf16[4,8,32,1024]{3,2,0,1:T(8,128)(2,1)}), bf16[4,8,32,1024]{3,2,0,1:T(8,128)(2,1)}, u32[]{:S(2)}, u32[]{:S(2)}) %all-to-all-start.1) | async-done | bytes 2097184 | tf_op jit(solution)/shard_map/all_to_all | solution.py:57
  636.5 1.8 copy.34
  638.3 2.8 gather_fusion
  641.1 73.8 %all-reduce.2.cloned.1.call-done = bf16[512,4096]{1,0:T(8,128)(2,1)} async-done(((bf16[512,4096]{1,0:T(8,128)(2,1)}), bf16[512,4096]{1,0:T(8,128)(2,1)}) %all-reduce.2.cloned.1.call-update) | async-done | bytes 4194320 | tf_op jit(solution)/shard_map/psum | solution.py:86
  714.9 5.0 fusion.3
  719.9 1.9 copy-done.2
  721.8 0.8 constant_dynamic-slice_fusion
  722.7 51.0 %all-gather.14.cloned.1.call-done = bf16[4096,1024]{1,0:T(8,128)(2,1)} async-done(((bf16[1024,1024]{1,0:T(8,128)(2,1)}), bf16[4096,1024]{1,0:T(8,128)(2,1)}) %all-gather.14.cloned.1.call-update) | async-done | bytes 8388624 | tf_op jit(solution)/shard_map/all_gather | solution.py:92
  773.7 10.6 %multiply_reduce_fusion = (f32[512]{0:T(512)S(1)}, f32[512,1024]{1,0:T(8,128)}) fusion(bf16[512,1024]{1,0:T(8,128)(2,1)S(1)} %copy-done.4, pred[512]{0:T(512)(128)(4,1)S(1)} %get-tuple-element.3, bf16[512,4096]{1,0:T(8,128)(2,1)} %copy-done.2, bf16[4096,1024]{1,0:T(8,128)(2,1)} %all-gather.14.cloned.1.call-done), kind=kOutput, calls=%fused_computation.14 | convolution fusion | flops 4297588224 | bytes 15731200 | tf_op jit(solution)/shard_map/dot_general | solution.py:91
  784.3 21.3 %psum.15 = f32[512]{0:T(512)S(1)} all-reduce(f32[512]{0:T(512)S(1)} %get-tuple-element.7), channel_id=1, replica_groups=mesh['dp'=4,'tensor'=8] {'tensor'}, use_global_device_ids=true, to_apply=%region_8.9 | all-reduce | flops 512 | bytes 4096 | tf_op jit(solution)/shard_map/psum | solution.py:96
  805.6 0.6 broadcast_multiply_fusion
  (40 shorter events, 2.9 us)
Async XLA Ops:
  7.2 2.9 copy-start
  7.2 80.2 %all-gather.6.cloned.1.call-start = ((), (), s32[]{:S(2)}) async-start(), calls=%async_computation.3 | async-start | bytes 4718592 | tf_op jit(solution)/shard_map/all_gather | solution.py:69
  7.9 173.3 %all-gather.8.cloned.1.call-start = ((), (), s32[]{:S(2)}) async-start(), calls=%async_computation.4 | async-start | bytes 18350080 | tf_op jit(solution)/shard_map/all_gather | solution.py:79
  8.7 268.1 %all-gather.12.cloned.1.call-start = ((), (), s32[]{:S(2)}) async-start(), calls=%async_computation.6 | async-start | bytes 18350080 | tf_op jit(solution)/shard_map/all_gather | solution.py:83
  9.4 362.8 %all-gather.10.cloned.1.call-start = ((), (), s32[]{:S(2)}) async-start(), calls=%async_computation.5 | async-start | bytes 18350080 | tf_op jit(solution)/shard_map/all_gather | solution.py:80
  10.0 513.2 %reduce-scatter.2.cloned.1.call-start = ((), (), s32[]{:S(2)}) async-start(), calls=%async_computation.9 | async-start | bytes 9437184 | tf_op jit(solution)/shard_map/reduce_scatter | solution.py:27
  26.8 0.7 copy-start.6
  26.8 688.0 %all-reduce.2.cloned.1.call-start = ((), (), s32[]{:S(2)}) async-start(), calls=%async_computation.7 | async-start | bytes 8388608 | tf_op jit(solution)/shard_map/psum | solution.py:86
  401.0 0.8 copy-start.5
  401.0 0.8 copy-start.7
  401.0 122.2 %copy-start.3 = (bf16[64,8192]{1,0:T(8,128)(2,1)S(1)}, bf16[64,8192]{1,0:T(8,128)(2,1)}, u32[]{:S(2)}) copy-start(bf16[64,8192]{1,0:T(8,128)(2,1)} %param.13) | copy-start | bytes 3145732
  401.0 372.7 %all-gather.14.cloned.1.call-start = ((), (), s32[]{:S(2)}) async-start(), calls=%async_computation.8 | async-start | bytes 10485760 | tf_op jit(solution)/shard_map/all_gather | solution.py:92
  559.1 77.3 %all-to-all-start.1 = ((bf16[4,8,32,1024]{3,2,0,1:T(8,128)(2,1)}), bf16[4,8,32,1024]{3,2,0,1:T(8,128)(2,1)}, u32[]{:S(2)}, u32[]{:S(2)}) async-start(bf16[4,8,32,1024]{3,2,0,1:T(8,128)(2,1)} %copy.33), calls=%async_computation.2 | async-start | bytes 4194304 | tf_op jit(solution)/shard_map/all_to_all | solution.py:57
  641.1 132.7 %copy-start.4 = (bf16[512,1024]{1,0:T(8,128)(2,1)S(1)}, bf16[512,1024]{1,0:T(8,128)(2,1)}, u32[]{:S(2)}) copy-start(bf16[512,1024]{1,0:T(8,128)(2,1)} %gather_fusion) | copy-start | bytes 3145732
  719.9 2.0 copy-start.2
  773.7 32.5 %copy-start.1 = (bf16[512,1024]{1,0:T(8,128)(2,1)S(1)}, bf16[512,1024]{1,0:T(8,128)(2,1)}, u32[]{:S(2)}) copy-start(bf16[512,1024]{1,0:T(8,128)(2,1)} %param.11) | copy-start | bytes 3145732
Sparse Core Ops, SparseCore 0:
  10.0 77.3 all-gather.5
  89.0 92.1 all-gather.7
  182.8 93.9 all-gather.11
  278.2 93.9 all-gather.9
  375.7 147.4 reduce-scatter.1
  526.7 188.0 all-reduce.1
  716.4 57.2 all-gather.13
where the time goes:
time: 814 us; the launch traced here: 813 us
  waiting for transfers between devices  639 us (79%)
  matrix products  72.8 us (9%)
  blocking collectives  49.5 us (6%)
  local copies, waits for them, and re-layouts  20.5 us (3%)
  between operations  14.3 us (2%)
  other arithmetic  12.4 us (2%)
    reduce_scatter x1, waiting for transfers between devices, local(): lax.psum_scatter(jnp.dot(portion, w_out, preferred_element_type=jnp.float...  119 us
    all_gather x1, waiting for transfers between devices, local(): up_acts = add_rows(lax.all_gather(w_up, 'dp', axis=0, tiled=True))  95.4 us
    all_gather x1, waiting for transfers between devices, local(): gate_acts = add_rows(lax.all_gather(w_gate, 'dp', axis=0, tiled=True))  90.7 us
    all_gather x1, waiting for transfers between devices, local(): lax.all_gather(w_down, 'dp', axis=1, tiled=True)  80.9 us
    psum x1, waiting for transfers between devices, local(): lax.psum(partial_sum.astype(jnp.bfloat16), 'tensor').astype(jnp.float32)  73.8 us
    all_to_all x1, waiting for transfers between devices, local(): lax.all_to_all(lax.all_to_all(send_blocks, 'dp', split_axis=0, concat_axi...  64.3 us
    all_gather x1, waiting for transfers between devices, local(): gathered = lax.all_gather(student_in, 'tensor', axis=1, tiled=True)  59.9 us
    all_gather x1, waiting for transfers between devices, local(): lax.all_gather(proj, 'dp', axis=0, tiled=True)  51 us
  transfers between devices with their start and end apart: 8, of which 8 were waited for; matrix products, arithmetic and copies ran while one was open for 11% of the time, Pallas kernels for 0%

commit v1 on v0

--- a/solution.py
+++ b/solution.py
@@ -83,7 +83,9 @@
         hidden, lax.all_gather(w_down, "dp", axis=1, tiled=True), preferred_element_type=jnp.float32
     )
     local_cols = student_in.shape[1]
-    mlp_sum = lax.psum(partial_sum.astype(jnp.bfloat16), "tensor").astype(jnp.float32)
+    mlp_sum = jnp.sum(lax.all_gather(partial_sum.astype(jnp.bfloat16), "tensor"), axis=0).astype(
+        jnp.float32
+    )
     out_full = (x_full + mlp_sum).astype(jnp.bfloat16)
     out_local = lax.dynamic_slice_in_dim(
         out_full, lax.axis_index("tensor") * local_cols, local_cols, 1

time: 814 us -> 1280 us (1.57)
  waiting for transfers between devices: 639 us -> 1090 us
  other arithmetic: 12.4 us -> 28.3 us
    all_gather x0 -> x1, waiting for transfers between devices: none -> 546 us  [local(): lax.all_gather(partial_sum.astype(jnp.bfloat16), 'tensor')]
    psum x1 -> x0, waiting for transfers between devices: 73.8 us -> none  [local(): lax.psum(partial_sum.astype(jnp.bfloat16), 'tensor').astype(jnp.float32)]
    reduce_sum x0 -> x1, other arithmetic: none -> 15.8 us  [local(): jnp.sum(lax.all_gather(partial_sum.astype(jnp.bfloat16), 'tensor'), axis=0)]
    all_gather x1, waiting for transfers between devices: 51 us -> 36.2 us  [local(): lax.all_gather(proj, 'dp', axis=0, tiled=True)]
  transfers between devices with their start and end apart: 8 -> 8, of which waited for: 8 -> 8; matrix products, arithmetic and copies ran while one was open for 11% -> 8% of each run, Pallas kernels for 0% -> 0%
where the time goes in v1:
time: 1280 us
  waiting for transfers between devices  1090 us (85%)
  matrix products  72.8 us (6%)
  blocking collectives  49.5 us (4%)
  other arithmetic  28.3 us (2%)
  local copies, waits for them, and re-layouts  20.5 us (2%)
  between operations  14.3 us (1%)
    all_gather x1, waiting for transfers between devices, local(): lax.all_gather(partial_sum.astype(jnp.bfloat16), 'tensor')  546 us
    reduce_scatter x1, waiting for transfers between devices, local(): lax.psum_scatter(jnp.dot(portion, w_out, preferred_element_type=jnp.float...  119 us
    all_gather x1, waiting for transfers between devices, local(): up_acts = add_rows(lax.all_gather(w_up, 'dp', axis=0, tiled=True))  95.4 us
    all_gather x1, waiting for transfers between devices, local(): gate_acts = add_rows(lax.all_gather(w_gate, 'dp', axis=0, tiled=True))  90.7 us
    all_gather x1, waiting for transfers between devices, local(): lax.all_gather(w_down, 'dp', axis=1, tiled=True)  81 us
    all_to_all x1, waiting for transfers between devices, local(): lax.all_to_all(lax.all_to_all(send_blocks, 'dp', split_axis=0, concat_axi...  60.9 us
    all_gather x1, waiting for transfers between devices, local(): gathered = lax.all_gather(student_in, 'tensor', axis=1, tiled=True)  59.9 us
    all_gather x1, waiting for transfers between devices, local(): lax.all_gather(proj, 'dp', axis=0, tiled=True)  36.2 us
  transfers between devices with their start and end apart: 8, of which 8 were waited for; matrix products, arithmetic and copies ran while one was open for 8% of the time, Pallas kernels for 0%

profile of v1, /device:TPU:0, one launch (start us, length us, event | category | flops | bytes accessed | tf_op | source)
XLA Modules:
  0.0 1283.0 jit_solution(9101830089235616560)
XLA Ops:
  7.2 0.7 all-gather.8.cloned.1.call-update
  8.0 0.7 all-gather.10.cloned.1.call-update
  8.7 0.7 all-gather.14.cloned.1.call-update
  10.0 16.8 %convolution_convert_fusion = bf16[512,8192]{1,0:T(8,128)(2,1)} fusion(bf16[512,1024]{1,0:T(8,128)(2,1)S(1)} %copy-done, bf16[1024,8192]{1,0:T(8,128)(2,1)} %param.12), kind=kOutput, calls=%fused_computation.5 | convolution fusion | flops 8594128896 | bytes 26214400 | tf_op jit(solution)/shard_map/dot_general | solution.py:28
  27.5 59.9 %all-gather.8.cloned.1.call-done = bf16[512,4096]{1,0:T(8,128)(2,1)} async-done(((bf16[512,512]{1,0:T(8,128)(2,1)}), bf16[512,4096]{1,0:T(8,128)(2,1)}) %all-gather.8.cloned.1.call-update) | async-done | bytes 4194320 | tf_op jit(solution)/shard_map/all_gather | solution.py:69
  87.4 3.1 fusion
  90.5 90.7 %all-gather.10.cloned.1.call-done = bf16[4096,1792]{1,0:T(8,128)(2,1)} async-done(((bf16[1024,1792]{1,0:T(8,128)(2,1)}), bf16[4096,1792]{1,0:T(8,128)(2,1)}) %all-gather.10.cloned.1.call-update) | async-done | bytes 14680080 | tf_op jit(solution)/shard_map/all_gather | solution.py:79
  181.2 14.6 %fusion.11 = f32[512,1792]{1,0:T(8,128)} fusion(bf16[4096,1792]{1,0:T(8,128)(2,1)} %all-gather.10.cloned.1.call-done, bf16[512,4096]{1,0:T(8,128)(2,1)} %all-gather.8.cloned.1.call-done, f32[4096]{0:T(1024)S(1)} %convert_element_type.49, f32[512]{0:T(512)S(1)} %add_rsqrt_fusion), kind=kOutput, calls=%fused_computation.23 | convolution fusion | flops 7524581376 | bytes 22562816 | tf_op jit(solution)/shard_map/dot_general | solution.py:77
  195.8 81.0 %all-gather.14.cloned.1.call-done = bf16[1792,4096]{1,0:T(8,128)(2,1)} async-done(((bf16[1792,1024]{1,0:T(8,128)(2,1)}), bf16[1792,4096]{1,0:T(8,128)(2,1)}) %all-gather.14.cloned.1.call-update) | async-done | bytes 14680080 | tf_op jit(solution)/shard_map/all_gather | solution.py:83
  276.8 95.4 %all-gather.12.cloned.1.call-done = bf16[4096,1792]{1,0:T(8,128)(2,1)} async-done(((bf16[1024,1792]{1,0:T(8,128)(2,1)}), bf16[4096,1792]{1,0:T(8,128)(2,1)}) %all-gather.12.cloned.1.call-update) | async-done | bytes 14680080 | tf_op jit(solution)/shard_map/all_gather | solution.py:80
  372.2 28.8 %convolution_convert_fusion.2 = bf16[512,4096]{1,0:T(8,128)(2,1)} fusion(bf16[1792,4096]{1,0:T(8,128)(2,1)} %all-gather.14.cloned.1.call-done, f32[512,1792]{1,0:T(8,128)} %fusion.11, bf16[4096,1792]{1,0:T(8,128)(2,1)} %all-gather.12.cloned.1.call-done, bf16[512,4096]{1,0:T(8,128)(2,1)} %all-gather.8.cloned.1.call-done, f32[4096]{0:T(1024)S(1)} %convert_element_type.49, ...), kind=kOutput, calls=%fused_computation.11 | convolution fusion | flops 15048376320 | bytes 41437184 | tf_op jit(solution)/shard_map/dot_general | solution.py:82
  402.0 1.7 select_reduce_fusion
  403.9 119.3 %reduce-scatter.2.cloned.1.call-done = bf16[64,8192]{1,0:T(8,128)(2,1)} async-done(((bf16[512,8192]{1,0:T(8,128)(2,1)}), bf16[64,8192]{1,0:T(8,128)(2,1)}) %reduce-scatter.2.cloned.1.call-update) | async-done | bytes 1048592 | tf_op jit(solution)/shard_map/reduce_scatter | solution.py:27
  523.2 1.7 multiply_reduce_fusion.1
  524.9 2.0 convolution_convert_fusion.1
  526.9 1.4 copy.35
  528.3 1.2 copy.37
  529.5 28.2 %all_to_all.10 = bf16[4,8,32,1024]{3,2,1,0:T(8,128)(2,1)S(1)} all-to-all(bf16[4,8,32,1024]{3,2,1,0:T(8,128)(2,1)S(1)} %bitcast.19), channel_id=1, replica_groups=mesh['dp'=4,'tensor'=8] {'dp'}, dimensions={0} | all-to-all | bytes 4194304 | tf_op jit(solution)/shard_map/all_to_all | solution.py:58
  557.7 1.5 copy.33
  559.1 4.4 all-to-all-start.1
  563.7 8.3 scatter_custom_fusion
  572.2 60.9 %all-to-all-done.1 = bf16[4,8,32,1024]{3,2,0,1:T(8,128)(2,1)} async-done(((bf16[4,8,32,1024]{3,2,0,1:T(8,128)(2,1)}), bf16[4,8,32,1024]{3,2,0,1:T(8,128)(2,1)}, u32[]{:S(2)}, u32[]{:S(2)}) %all-to-all-start.1) | async-done | bytes 2097184 | tf_op jit(solution)/shard_map/all_to_all | solution.py:57
  633.0 1.8 copy.34
  634.9 2.8 gather_fusion
  637.6 546.2 %all-gather.18.cloned.1.call-done = bf16[4096,4096]{1,0:T(8,128)(2,1)} async-done(((bf16[512,4096]{1,0:T(8,128)(2,1)}), bf16[4096,4096]{1,0:T(8,128)(2,1)}) %all-gather.18.cloned.1.call-update) | async-done | bytes 33554448 | tf_op jit(solution)/shard_map/all_gather | solution.py:86
  1183.8 15.8 %reduce_sum.49 = bf16[512,4096]{1,0:T(8,128)(2,1)} reduce(bf16[8,512,4096]{2,1,0:T(8,128)(2,1)} %bitcast.16, bf16[]{:T(256)} %constant.63.clone.1), dimensions={0}, to_apply=%region_1.0 | reduce | flops 14680064 | bytes 37748736 | tf_op jit(solution)/shard_map/reduce_sum | solution.py:86
  1199.6 5.1 fusion.3
  1204.7 1.9 copy-done.2
  1206.6 0.8 constant_dynamic-slice_fusion
  1207.5 36.2 %all-gather.16.cloned.1.call-done = bf16[4096,1024]{1,0:T(8,128)(2,1)} async-done(((bf16[1024,1024]{1,0:T(8,128)(2,1)}), bf16[4096,1024]{1,0:T(8,128)(2,1)}) %all-gather.16.cloned.1.call-update) | async-done | bytes 8388624 | tf_op jit(solution)/shard_map/all_gather | solution.py:94
  1243.7 10.6 multiply_reduce_fusion
  1254.3 21.3 %psum.7 = f32[512]{0:T(512)S(1)} all-reduce(f32[512]{0:T(512)S(1)} %get-tuple-element.7), channel_id=1, replica_groups=mesh['dp'=4,'tensor'=8] {'tensor'}, use_global_device_ids=true, to_apply=%region_8.9 | all-reduce | flops 512 | bytes 4096 | tf_op jit(solution)/shard_map/psum | solution.py:98
  (41 shorter events, 3.4 us)
Async XLA Ops:
  7.2 2.9 copy-start
  7.2 80.2 %all-gather.8.cloned.1.call-start = ((), (), s32[]{:S(2)}) async-start(), calls=%async_computation.3 | async-start | bytes 4718592 | tf_op jit(solution)/shard_map/all_gather | solution.py:69
  7.9 173.3 %all-gather.10.cloned.1.call-start = ((), (), s32[]{:S(2)}) async-start(), calls=%async_computation.4 | async-start | bytes 18350080 | tf_op jit(solution)/shard_map/all_gather | solution.py:79
  8.7 268.1 %all-gather.14.cloned.1.call-start = ((), (), s32[]{:S(2)}) async-start(), calls=%async_computation.6 | async-start | bytes 18350080 | tf_op jit(solution)/shard_map/all_gather | solution.py:83
  9.4 362.8 %all-gather.12.cloned.1.call-start = ((), (), s32[]{:S(2)}) async-start(), calls=%async_computation.5 | async-start | bytes 18350080 | tf_op jit(solution)/shard_map/all_gather | solution.py:80
  10.0 513.2 %reduce-scatter.2.cloned.1.call-start = ((), (), s32[]{:S(2)}) async-start(), calls=%async_computation.8 | async-start | bytes 9437184 | tf_op jit(solution)/shard_map/reduce_scatter | solution.py:27
  26.8 0.7 copy-start.6
  26.8 1157.0 %all-gather.18.cloned.1.call-start = ((), (), s32[]{:S(2)}) async-start(), calls=%async_computation.9 | async-start | bytes 37748736 | tf_op jit(solution)/shard_map/all_gather | solution.py:86
  401.0 0.8 copy-start.5
  401.0 0.8 copy-start.7
  401.0 122.2 %copy-start.3 = (bf16[64,8192]{1,0:T(8,128)(2,1)S(1)}, bf16[64,8192]{1,0:T(8,128)(2,1)}, u32[]{:S(2)}) copy-start(bf16[64,8192]{1,0:T(8,128)(2,1)} %param.13) | copy-start | bytes 3145732
  401.1 842.6 %all-gather.16.cloned.1.call-start = ((), (), s32[]{:S(2)}) async-start(), calls=%async_computation.7 | async-start | bytes 10485760 | tf_op jit(solution)/shard_map/all_gather | solution.py:94
  559.1 73.9 %all-to-all-start.1 = ((bf16[4,8,32,1024]{3,2,0,1:T(8,128)(2,1)}), bf16[4,8,32,1024]{3,2,0,1:T(8,128)(2,1)}, u32[]{:S(2)}, u32[]{:S(2)}) async-start(bf16[4,8,32,1024]{3,2,0,1:T(8,128)(2,1)} %copy.33), calls=%async_computation.2 | async-start | bytes 4194304 | tf_op jit(solution)/shard_map/all_to_all | solution.py:57
  1199.6 44.0 %copy-start.4 = (bf16[512,1024]{1,0:T(8,128)(2,1)S(1)}, bf16[512,1024]{1,0:T(8,128)(2,1)}, u32[]{:S(2)}) copy-start(bf16[512,1024]{1,0:T(8,128)(2,1)} %gather_fusion) | copy-start | bytes 3145732
  1204.7 1.9 copy-start.2
  1243.7 32.5 %copy-start.1 = (bf16[512,1024]{1,0:T(8,128)(2,1)S(1)}, bf16[512,1024]{1,0:T(8,128)(2,1)}, u32[]{:S(2)}) copy-start(bf16[512,1024]{1,0:T(8,128)(2,1)} %param.11) | copy-start | bytes 3145732
Sparse Core Ops, SparseCore 0:
  10.0 77.3 all-gather.7
  89.0 92.1 all-gather.9
  182.8 93.9 all-gather.13
  278.2 93.9 all-gather.11
  375.7 147.4 reduce-scatter.1
  524.6 659.2 all-gather.17
  1185.4 58.2 all-gather.15
